TPU v7x, 512 devices: a whole 4x8x8 slice. The times are simulated.
512 devices in a mesh: section: 8 (over y), freq: 64 (over z, x, core).
Axes of the slice: x: 4, y: 8, z: 8, core: 2. Of those that a mesh axis runs over, the one named last changes fastest.
Arguments:
- spectra: float32 [16, 16, 524288], P('section', None, 'freq'), may hold values from 0.1 to 90, as said below
- channel_gain: float32 [524288], P('freq'), may hold values from 0.5 to 2
- bandpass_bin: int32 [524288], P('freq'), may hold values from 0 to 255, never falling along the last dimension, each value on 1 to 8192 neighbouring positions
- drift_range: int32 [16], replicated, may hold values from 1 to 8, as said below
- hit_cutoff: int32 [16, 8, 16], replicated, may hold values from 0 to 1023
Outputs:
- drift_score: float32 [16, 8, 524288], P(None, 'section', 'freq')
Inputs may be any that keep to these rules, and one draw needn't show every extreme that they name: `spectra`: every entry is positive. `bandpass_bin`: the bins never fall along the channels and each of the 256 bins holds 1 to 8192 channels. `drift_range`: some group reaches 8 and some other group searches stride 1 only.
All inputs are finite; a program needn't handle non-finite values.
Results may differ from a plain program's by a relative error of at most 0.0003.
Values sent between devices are 32-bit elements; how exact they have to be, the bound alone decides.
A program may use at most 64 MiB of HBM per device.

v0:
```python
import jax
import jax.numpy as jnp
from jax import lax
from jax.sharding import PartitionSpec as P


def copy_for_each(x, axis):
    copies = jnp.broadcast_to(x, (lax.axis_size(axis), *x.shape))
    return lax.all_to_all(copies, axis, split_axis=0, concat_axis=0, tiled=True)


def over_copies(x, axis):
    return copy_for_each(x, axis).sum(axis=0)


def packed_total(arrays, axis):
    ends = [0]
    for a in arrays:
        ends.append(ends[-1] + a.size)
    subtotal = over_copies(jnp.concatenate([a.ravel() for a in arrays]), axis)
    return tuple((subtotal[b:e].reshape(a.shape) for a, b, e in zip(arrays, ends, ends[1:])))


def all_in_one(x, axis):
    leaves = jax.tree.leaves(x)
    turns = sorted(range(len(leaves)), key=lambda k: -leaves[k].size)
    width = (1, *leaves[turns[0]].shape)[-1]
    lines = [
        jnp.pad(leaves[k].reshape(-1), (0, -leaves[k].size % width)).reshape(-1, width)
        for k in turns
    ]
    both, at, found = (copy_for_each(jnp.concatenate(lines), axis), 0, {})
    for k, line in zip(turns, lines):
        slab = both[:, at : at + len(line)].reshape(len(both), -1)
        found[k] = slab[:, : leaves[k].size].reshape(-1, *leaves[k].shape)
        at += len(line)
    numbers = iter(range(len(leaves)))
    return jax.tree.map(lambda _: found[next(numbers)], x)


def folded_in_pairs(pieces, combine):
    while len(jax.tree.leaves(pieces)[0]) > 1:
        pieces = jax.vmap(combine)(
            *(jax.tree.map(lambda part: part[side::2], pieces) for side in (0, 1))
        )
    return jax.tree.map(lambda part: part[0], pieces)


def prefix(x, axis, combine, identity):
    length, position = (lax.axis_size(axis), lax.axis_index(axis))
    passed = jnp.arange(length) < position

    def kept(part, zero, own):
        part = jnp.where(
            passed.reshape(-1, *(1 for _ in own.shape)), part, jnp.asarray(zero, own.dtype)
        )
        return part

    pieces = all_in_one(x, axis)
    return folded_in_pairs(jax.tree.map(kept, pieces, identity, x), combine)


def passed_along(block, axis, distance):
    devices = range(lax.axis_size(axis))
    route = [(i - distance, i) for i in devices if i - distance in devices]
    return lax.ppermute(block, axis, route)


def taylor_tree(extended, stride, margin):
    length = extended.shape[-1]
    current = extended[:, None, :]
    blocks_width = 1
    while current.shape[0] > 1:
        former = current[0::2]
        latter = jnp.pad(current[1::2], ((0, 0), (0, 0), (0, margin)))
        merged = []
        for half_idx in range(blocks_width):
            anchor = former[:, half_idx]
            source = latter[:, half_idx]
            merged.append(
                anchor + lax.dynamic_slice_in_dim(source, half_idx * stride, length, axis=1)
            )
            merged.append(
                anchor + lax.dynamic_slice_in_dim(source, (half_idx + 1) * stride, length, axis=1)
            )
        current = jnp.stack(merged, axis=1)
        blocks_width = blocks_width * 2
    return current[0]


def score_rate(extended, stride, cut_row, chan_dev, margin):
    drifts = taylor_tree(extended, stride, margin)[:, :chan_dev]
    cut_levels = cut_row.astype(jnp.float32) / 256.0
    return jnp.mean(jax.nn.relu(0.25 * drifts - cut_levels[:, None]), axis=0)


def block_layout(chan_dev):
    width = min(1024, chan_dev)
    return (width, chan_dev // width)


def bin_partials(summed, bandpass_bin, total_bins, integrations):
    group_dev, chan_dev = summed.shape
    width, blocks = block_layout(chan_dev)
    bins_iota = jnp.arange(total_bins, dtype=jnp.int32)
    values = jnp.transpose(summed.reshape(group_dev, blocks, width), (1, 0, 2))
    indices = bandpass_bin.reshape(blocks, width)

    def bin_one_block(carry, items):
        block_values, block_index = items
        one_hot = (block_index[:, None] == bins_iota[None, :]).astype(jnp.float32)
        sums = carry[0] + jnp.dot(
            block_values,
            one_hot,
            precision=lax.Precision.HIGHEST,
            preferred_element_type=jnp.float32,
        )
        counts = carry[1] + jnp.sum(one_hot, axis=0)
        return ((sums, counts), None)

    start = (jnp.zeros((group_dev, total_bins), jnp.float32), jnp.zeros((total_bins,), jnp.float32))
    (bin_sums, counts), unused = lax.scan(bin_one_block, start, (values, indices))
    tallies = jnp.broadcast_to(float(integrations) * counts[None, :], bin_sums.shape)
    return (bin_sums, tallies)


def read_levels(running, bandpass_bin):
    group_dev, total_bins = running.shape
    chan_dev = bandpass_bin.shape[0]
    width, blocks = block_layout(chan_dev)
    bins_iota = jnp.arange(total_bins, dtype=jnp.int32)

    def read_one_block(carry, block_index):
        one_hot = (block_index[:, None] == bins_iota[None, :]).astype(jnp.float32)
        picked = lax.dot_general(
            running,
            one_hot,
            (((1,), (1,)), ((), ())),
            precision=lax.Precision.HIGHEST,
            preferred_element_type=jnp.float32,
        )
        return (carry, picked)

    unused, picked_blocks = lax.scan(read_one_block, 0, bandpass_bin.reshape(blocks, width))
    return jnp.transpose(picked_blocks, (1, 0, 2)).reshape(group_dev, chan_dev)


def add_pair(earlier, later):
    return (earlier[0] + later[0], earlier[1] + later[1])


def shards(spectra, channel_gain, bandpass_bin, drift_range, hit_cutoff):
    group_dev, integrations, chan_dev = spectra.shape
    total_bins = 4 * lax.axis_size("freq")
    calibrated = spectra * channel_gain[None, None, :]
    summed = jnp.sum(calibrated, axis=1)
    bin_sums, tallies = bin_partials(summed, bandpass_bin, total_bins, integrations)
    freq_sums, freq_tallies = packed_total((bin_sums, tallies), "freq")
    zero_row = jnp.zeros((total_bins,), jnp.float32)
    before_sums, before_tallies = prefix(
        (jnp.sum(freq_sums, axis=0), jnp.sum(freq_tallies, axis=0)),
        "section",
        add_pair,
        (zero_row, zero_row),
    )
    running = (before_sums[None, :] + jnp.cumsum(freq_sums, axis=0)) / (
        before_tallies[None, :] + jnp.cumsum(freq_tallies, axis=0)
    )
    levels = read_levels(running, bandpass_bin)
    normal = calibrated / levels[:, None, :] - 1.0
    rate_count = hit_cutoff.shape[1]
    margin = rate_count * (integrations - 1)
    right_rim = passed_along(normal[:, :, :margin], "freq", -1)
    section_first = lax.axis_index("section") * group_dev

    def one_group(position, scores):
        extended = jnp.concatenate([normal[position], right_rim[position]], axis=1)
        group_id = section_first + position
        for stride in range(1, rate_count + 1):
            result_row = lax.cond(
                stride <= drift_range[group_id],
                lambda: score_rate(
                    extended, stride, hit_cutoff[group_id, stride - 1], chan_dev, margin
                ),
                lambda: jnp.zeros((chan_dev,), jnp.float32),
            )
            scores = scores.at[position, stride - 1].set(result_row)
        return scores

    own_scores = lax.fori_loop(
        0, group_dev, one_group, jnp.zeros((group_dev, rate_count, chan_dev), jnp.float32)
    )
    return lax.all_to_all(own_scores, "section", split_axis=1, concat_axis=0, tiled=True)


def solution(mesh):
    return jax.shard_map(
        shards,
        mesh=mesh,
        in_specs=(P("section", None, "freq"), P("freq"), P("freq"), P(), P()),
        out_specs=P(None, "section", "freq"),
        check_vma=False,
    )
```

profile of v0, /device:TPU:1, one launch (start us, length us, event | category | flops | bytes accessed | tf_op | source)
XLA Modules:
  0.0 379.2 jit_solution(10079931983943855829)
XLA Ops:
  2.3 6.1 %while.47 = (s32[]{:T(128)}, f32[2,256]{1,0:T(2,128)S(1)}, f32[256]{0:T(256)S(1)}, f32[8,2,1024]{2,1,0:T(2,128)S(1)}, s32[8,1024]{1,0:T(8,128)S(1)}, /*index=5*/s32[]{:T(128)}, s32[]{:T(128)}) while((s32[]{:T(128)}, f32[2,256]{1,0:T(2,128)S(1)}, f32[256]{0:T(256)S(1)}, f32[8,2,1024]{2,1,0:T(2,128)S(1)}, s32[8,1024]{1,0:T(8,128)S(1)}, ...), condition=%wide.region_3.4_spmd.clone, body=%wide.region_1.3_spmd.clone.sunk | while | flops 7341315 | bytes 32864 | solution.py:122
  9.3 15.0 %all-to-all-start = ((f32[64,1,1024]{2,1,0:T(1,128)}), f32[64,1,1024]{2,1,0:T(1,128)S(1)}, u32[]{:S(2)}, u32[]{:S(2)}) async-start(f32[64,1,1024]{2,1,0:T(1,128)} %broadcast_in_dim.95), calls=%async_computation | async-start | bytes 524288 | tf_op jit(solution)/shard_map/all_to_all | solution.py:9
  24.3 13.1 %all-to-all-done = f32[64,1,1024]{2,1,0:T(1,128)S(1)} async-done(((f32[64,1,1024]{2,1,0:T(1,128)}), f32[64,1,1024]{2,1,0:T(1,128)S(1)}, u32[]{:S(2)}, u32[]{:S(2)}) %all-to-all-start) | async-done | bytes 262176 | tf_op jit(solution)/shard_map/all_to_all | solution.py:9
  38.2 6.8 %all-to-all-start.1 = ((f32[8,2,256]{2,1,0:T(2,128)}), f32[8,2,256]{2,1,0:T(2,128)S(1)}, u32[]{:S(2)}, u32[]{:S(2)}) async-start(f32[8,2,256]{2,1,0:T(2,128)} %broadcast_in_dim.96), calls=%async_computation.1 | async-start | bytes 32768 | tf_op jit(solution)/shard_map/all_to_all | solution.py:9
  45.1 6.5 %all-to-all-done.1 = f32[8,2,256]{2,1,0:T(2,128)S(1)} async-done(((f32[8,2,256]{2,1,0:T(2,128)}), f32[8,2,256]{2,1,0:T(2,128)S(1)}, u32[]{:S(2)}, u32[]{:S(2)}) %all-to-all-start.1) | async-done | bytes 16416 | tf_op jit(solution)/shard_map/all_to_all | solution.py:9
  52.0 5.2 %while.46 = (s32[]{:T(128)}, f32[8,2,1024]{2,1,0:T(2,128)S(1)}, s32[8,1024]{1,0:T(8,128)S(1)}, f32[2,256]{1,0:T(2,128)S(1)}, s32[]{:T(128)}) while((s32[]{:T(128)}, f32[8,2,1024]{2,1,0:T(2,128)S(1)}, s32[8,1024]{1,0:T(8,128)S(1)}, f32[2,256]{1,0:T(2,128)S(1)}, s32[]{:T(128)}) %tuple.567), condition=%wide.region_10.11_spmd.clone, body=%wide.region_9.10_spmd.clone.sunk | while | flops 6553602 | bytes 22597 | solution.py:144
  57.3 3.6 collective-permute-start
  61.0 1.9 collective-permute-done
  62.9 228.3 %while.45 = (s32[]{:T(128)}, f32[2,8,8192]{2,1,0:T(8,128)S(1)}, s32[]{:T(128)}, s32[16]{0:T(128)S(1)}, f32[2,16,8192]{2,1,0:T(8,128)S(1)}, /*index=5*/f32[2,16,1...) while((s32[]{:T(128)}, f32[2,8,8192]{2,1,0:T(8,128)S(1)}, ...), condition=%wide.region_44.45_spmd, body=%wide.region_11.44_spmd.sunk | while | flops 12904750 | bytes 129848776 | solution.py:190
  64.5 17.2 %conditional.16 = (f32[1,1,8192]{2,1,0:T(1,128)S(1)}) conditional(s32[]{:T(128)} %bitcast.1205, () %tuple.531, (f32[16,8312]{1,0:T(8,128)S(1)}, s32[]{:T(128)}, s32[16,8,16]{2,1,0:T(8,128)}) %tuple.532), branch_computations={%region_13.13_spmd, %region_14.15_spmd} | conditional | flops 1588258 | bytes 15801198 | solution.py:180
  68.4 1.7 slice.1122
  70.4 2.2 slice.1130
  72.7 2.2 slice.1128
  77.7 3.0 stack.577
  83.9 17.8 %conditional.17 = (f32[1,1,8192]{2,1,0:T(1,128)S(1)}) conditional(s32[]{:T(128)} %bitcast.1207, () %tuple.533, (f32[16,8312]{1,0:T(8,128)S(1)}, s32[]{:T(128)}, s32[16,8,16]{2,1,0:T(8,128)}) %tuple.532), branch_computations={%region_17.17_spmd, %region_18.19_spmd} | conditional | flops 1588258 | bytes 15801198 | solution.py:180
  88.3 1.7 slice.1158
  90.4 2.2 slice.1166
  92.6 2.2 slice.1164
  97.7 3.0 stack.611
  103.1 17.4 %conditional.18 = (f32[1,1,8192]{2,1,0:T(1,128)S(1)}) conditional(s32[]{:T(128)} %bitcast.1208, () %tuple.534, (f32[16,8312]{1,0:T(8,128)S(1)}, s32[]{:T(128)}, s32[16,8,16]{2,1,0:T(8,128)}) %tuple.532), branch_computations={%region_21.21_spmd, %region_22.23_spmd} | conditional | flops 1588258 | bytes 15801198 | solution.py:180
  106.9 1.7 slice.1194
  109.0 2.2 slice.1202
  111.2 2.2 slice.1200
  116.3 3.0 stack.645
  122.7 17.2 %conditional.19 = (f32[1,1,8192]{2,1,0:T(1,128)S(1)}) conditional(s32[]{:T(128)} %bitcast.1209, () %tuple.535, (f32[16,8312]{1,0:T(8,128)S(1)}, s32[]{:T(128)}, s32[16,8,16]{2,1,0:T(8,128)}) %tuple.532), branch_computations={%region_25.25_spmd, %region_26.27_spmd} | conditional | flops 1588258 | bytes 15801198 | solution.py:180
  126.6 1.7 slice.1230
  128.7 2.2 slice.1238
  130.9 2.2 slice.1236
  136.0 3.0 stack.679
  141.4 17.2 %conditional.20 = (f32[1,1,8192]{2,1,0:T(1,128)S(1)}) conditional(s32[]{:T(128)} %bitcast.1210, () %tuple.536, (f32[16,8312]{1,0:T(8,128)S(1)}, s32[]{:T(128)}, s32[16,8,16]{2,1,0:T(8,128)}) %tuple.532), branch_computations={%region_29.29_spmd, %region_30.31_spmd} | conditional | flops 1588258 | bytes 15801198 | solution.py:180
  145.3 1.7 slice.1266
  147.4 2.2 slice.1274
  149.6 2.2 slice.1272
  154.7 3.0 stack.713
  160.1 17.2 %conditional.21 = (f32[1,1,8192]{2,1,0:T(1,128)S(1)}) conditional(s32[]{:T(128)} %bitcast.1211, () %tuple.537, (f32[16,8312]{1,0:T(8,128)S(1)}, s32[]{:T(128)}, s32[16,8,16]{2,1,0:T(8,128)}) %tuple.532), branch_computations={%region_33.33_spmd, %region_34.35_spmd} | conditional | flops 1588258 | bytes 15801198 | solution.py:180
  163.9 1.7 slice.1302
  166.0 2.2 slice.1310
  168.2 2.2 slice.1308
  173.3 3.0 stack.747
  178.9 17.2 %conditional.22 = (f32[1,1,8192]{2,1,0:T(1,128)S(1)}) conditional(s32[]{:T(128)} %bitcast.1212, () %tuple.538, (f32[16,8312]{1,0:T(8,128)S(1)}, s32[]{:T(128)}, s32[16,8,16]{2,1,0:T(8,128)}) %tuple.532), branch_computations={%region_37.37_spmd, %region_38.39_spmd} | conditional | flops 1588258 | bytes 15801198 | solution.py:180
  182.8 1.7 slice.1338
  184.9 2.2 slice.1346
  187.1 2.2 slice.1344
  192.2 3.0 stack.781
  197.5 17.6 %conditional.23 = (f32[1,1,8192]{2,1,0:T(1,128)S(1)}) conditional(s32[]{:T(128)} %bitcast.1213, () %tuple.539, (f32[16,8312]{1,0:T(8,128)S(1)}, s32[]{:T(128)}, s32[16,8,16]{2,1,0:T(8,128)}) %tuple.532), branch_computations={%region_41.41_spmd, %region_42.43_spmd} | conditional | flops 1588258 | bytes 15801198 | solution.py:180
  203.9 2.2 slice.1382
  206.1 2.2 slice.1380
  211.2 3.0 stack.815
  217.5 17.2 %conditional.16 = (f32[1,1,8192]{2,1,0:T(1,128)S(1)}) conditional(s32[]{:T(128)} %bitcast.1205, () %tuple.531, (f32[16,8312]{1,0:T(8,128)S(1)}, s32[]{:T(128)}, s32[16,8,16]{2,1,0:T(8,128)}) %tuple.532), branch_computations={%region_13.13_spmd, %region_14.15_spmd} | conditional | flops 1588258 | bytes 15801198 | solution.py:180
  221.4 1.7 slice.1122
  223.4 2.2 slice.1130
  225.7 2.2 slice.1128
  230.7 3.0 stack.577
  236.9 17.6 %conditional.17 = (f32[1,1,8192]{2,1,0:T(1,128)S(1)}) conditional(s32[]{:T(128)} %bitcast.1207, () %tuple.533, (f32[16,8312]{1,0:T(8,128)S(1)}, s32[]{:T(128)}, s32[16,8,16]{2,1,0:T(8,128)}) %tuple.532), branch_computations={%region_17.17_spmd, %region_18.19_spmd} | conditional | flops 1588258 | bytes 15801198 | solution.py:180
  241.1 1.7 slice.1158
  243.2 2.2 slice.1166
  245.4 2.2 slice.1164
  250.5 3.0 stack.611
  255.9 17.4 %conditional.18 = (f32[1,1,8192]{2,1,0:T(1,128)S(1)}) conditional(s32[]{:T(128)} %bitcast.1208, () %tuple.534, (f32[16,8312]{1,0:T(8,128)S(1)}, s32[]{:T(128)}, s32[16,8,16]{2,1,0:T(8,128)}) %tuple.532), branch_computations={%region_21.21_spmd, %region_22.23_spmd} | conditional | flops 1588258 | bytes 15801198 | solution.py:180
  261.9 2.2 slice.1202
  264.1 2.2 slice.1200
  269.2 3.0 stack.645
  281.7 2.8 conditional.23
  291.7 85.7 %all_to_all.30 = f32[2,8,8192]{2,0,1:T(2,128)S(1)} all-to-all(f32[2,8,8192]{2,0,1:T(2,128)S(1)} %copy.15), channel_id=1, replica_groups=mesh['section'=8,'freq'=64] {'section'}, dimensions={1} | all-to-all | bytes 1048576 | tf_op jit(solution)/shard_map/all_to_all | solution.py:193
  (452 shorter events, 126.4 us)
Async XLA Ops:
  0.0 0.8 copy-start.1
  9.3 47.9 %copy-start = (f32[2,16,8192]{2,1,0:T(8,128)S(1)}, f32[2,16,8192]{2,1,0:T(8,128)}, u32[]{:S(2)}) copy-start(f32[2,16,8192]{2,1,0:T(8,128)} %param.43) | copy-start | bytes 3145732
  9.3 28.0 %all-to-all-start = ((f32[64,1,1024]{2,1,0:T(1,128)}), f32[64,1,1024]{2,1,0:T(1,128)S(1)}, u32[]{:S(2)}, u32[]{:S(2)}) async-start(f32[64,1,1024]{2,1,0:T(1,128)} %broadcast_in_dim.95), calls=%async_computation | async-start | bytes 524288 | tf_op jit(solution)/shard_map/all_to_all | solution.py:9
  38.2 13.4 %all-to-all-start.1 = ((f32[8,2,256]{2,1,0:T(2,128)}), f32[8,2,256]{2,1,0:T(2,128)S(1)}, u32[]{:S(2)}, u32[]{:S(2)}) async-start(f32[8,2,256]{2,1,0:T(2,128)} %broadcast_in_dim.96), calls=%async_computation.1 | async-start | bytes 32768 | tf_op jit(solution)/shard_map/all_to_all | solution.py:9
  57.3 5.5 %collective-permute-start = (f32[2,16,120]{2,1,0:T(8,128)S(1)}, f32[2,16,120]{2,1,0:T(8,128)S(1)}, u32[]{:S(2)}, u32[]{:S(2)}) collective-permute-start(f32[2,16,120]{2,1,0:T(8,128)S(1)} %slice.1580), channel_id=1, source_target_pairs={{1,0},{2,1},{3,2},{4,3},{5,4},{6,5},{7,6},{8,7},{9,8},{10,9},{11,1... | collective-permute-start | bytes 46088 | tf_op jit(solution)/shard_map/ppermute | solution.py:66
  61.0 1.9 copy-start.2
  61.0 1.9 copy-start.3
where the time goes:
time: 377 us; the launch traced here: 379 us
  local copies, waits for them, and re-layouts  152 us (40%)
  blocking collectives  85.7 us (23%)
  other arithmetic  62.1 us (16%)
  starting transfers between devices  25.4 us (7%)
  loops' own time  23.6 us (6%)
  waiting for transfers between devices  21.5 us (6%)
  matrix products  8.85 us (2%)
    all_to_all x1, blocking collectives, shards(): lax.all_to_all(own_scores, 'section', split_axis=1, concat_axis=0, tiled=...  85.7 us
    slice x44, local copies, waits for them, and re-layouts, taylor_tree(): latter = jnp.pad(current[1::2], ((0, 0), (0, 0), (0, margin)))  55.6 us
    slice x33, local copies, waits for them, and re-layouts, taylor_tree(): former = current[0::2]  52.6 us
    another operation x11, local copies, waits for them, and re-layouts, taylor_tree(): current = jnp.stack(merged, axis=1)  33.3 us
    another operation x99, other arithmetic, taylor_tree(): current = jnp.stack(merged, axis=1)  22.9 us
    all_to_all x2, starting transfers between devices, copy_for_each(): return lax.all_to_all(copies, axis, split_axis=0, concat_axis=0, tiled=True)  21.8 us
    all_to_all x2, waiting for transfers between devices, copy_for_each(): return lax.all_to_all(copies, axis, split_axis=0, concat_axis=0, tiled=True)  19.6 us
    another operation x1, loops' own time, shards(): lax.fori_loop(0, group_dev, one_group, jnp.zeros((group_dev, rate_count,...  16.4 us
  transfers between devices with their start and end apart: 3, of which 3 were waited for; matrix products, arithmetic and copies ran while one was open for 0% of the time, Pallas kernels for 0%

commit v1 on v0

v1 whole, which is shorter than its diff:
```python
import functools

import jax
import jax.numpy as jnp
from jax import lax
from jax.experimental import pallas as pl
from jax.experimental.pallas import tpu as pltpu
from jax.sharding import PartitionSpec as P

F32 = jnp.float32
BF16 = jnp.bfloat16
LANES = 128
SUB = 8
MESH = pl.DeviceIdType.MESH


def remote(src, dst, send, recv, where):
    return pltpu.make_async_remote_copy(
        src_ref=src, dst_ref=dst, send_sem=send, recv_sem=recv, device_id=where, device_id_type=MESH
    )


def kernel(
    sizes,
    spec_hbm,
    gain_hbm,
    bins_hbm,
    reach_hbm,
    cut_hbm,
    out_ref,
    nat,
    gain,
    bins,
    reach,
    cut,
    halo,
    halo_gain,
    halo_bins,
    ext_gain,
    ext_bins,
    norm,
    quads,
    scores,
    part,
    near,
    near_sum,
    far,
    far_sum,
    early,
    load_sem,
    near_send,
    near_recv,
    far_send,
    far_recv,
    early_send,
    early_recv,
    halo_send,
    halo_recv,
    score_send,
    score_recv,
):
    ns, nf, nc, groups, integ, chans, total_bins = sizes
    nz = nf // nc
    width = chans // SUB
    cols = width // LANES
    rows = chans // LANES
    me = lax.axis_index("section")
    here = lax.axis_index("freq")
    z, xc = here // nc, here % nc

    near_peers = [z * nc + (xc + d) % nc for d in range(1, nc)]
    far_peers = [((z + d) % nz) * nc + xc for d in range(1, nz)]
    section_peers = [(me + d) % ns for d in range(1, ns)]
    left, right = (here + nf - 1) % nf, (here + 1) % nf

    loads = [
        pltpu.make_async_copy(bins_hbm, bins, load_sem.at[0]),
        pltpu.make_async_copy(gain_hbm, gain, load_sem.at[1]),
    ]
    loads += [
        pltpu.make_async_copy(spec_hbm.at[g], nat.at[g], load_sem.at[2 + g]) for g in range(groups)
    ]
    loads += [
        pltpu.make_async_copy(reach_hbm, reach, load_sem.at[2 + groups]),
        pltpu.make_async_copy(cut_hbm.at[pl.ds(groups * me, groups)], cut, load_sem.at[3 + groups]),
    ]
    for c in loads:
        c.start()

    barrier = pltpu.get_barrier_semaphore()
    for peer in near_peers + far_peers + [left, right]:
        pl.semaphore_signal(barrier, inc=1, device_id={"freq": peer}, device_id_type=MESH)
    for peer in section_peers:
        pl.semaphore_signal(barrier, inc=1, device_id={"section": peer}, device_id_type=MESH)

    for c in loads[: 2 + groups]:
        c.wait()
    acc = jnp.zeros((SUB, total_bins), F32)
    step = min(8, rows)
    bin_row = lax.broadcasted_iota(jnp.int32, (total_bins, LANES), 0)
    for r0 in range(0, rows, step):
        one_hot = jnp.concatenate(
            [(bin_row == bins[r : r + 1, :]).astype(F32).astype(BF16) for r in range(r0, r0 + step)],
            axis=1,
        )
        gain_row = jnp.concatenate([gain[r : r + 1, :] for r in range(r0, r0 + step)], axis=1)
        span = pl.ds(r0 * LANES, step * LANES)
        value = jnp.concatenate(
            [jnp.sum(nat[g, :, span], axis=0, keepdims=True) for g in range(groups)], axis=0
        )
        value = value * gain_row
        high = value.astype(BF16)
        rest = value - high.astype(F32)
        middle = rest.astype(BF16)
        low = rest - middle.astype(F32)
        lhs = jnp.concatenate(
            [high.astype(F32), middle.astype(F32), low, jnp.ones_like(value)], axis=0
        )
        acc = acc + lax.dot_general(
            lhs.astype(BF16), one_hot, (((1,), (1,)), ((), ())), preferred_element_type=F32
        )
    sums = acc[0:2] + acc[2:4] + acc[4:6]
    counts = acc[6:8]
    tile = jnp.concatenate(
        [sums[:, :LANES], counts[:, :LANES], sums[:, LANES:], counts[:, LANES:]], axis=0
    )
    part[...] = tile

    pl.semaphore_wait(barrier, nc + nz + ns - 1)

    near_copies = [
        remote(part, near.at[d], near_send.at[d], near_recv.at[d], {"freq": p})
        for d, p in enumerate(near_peers)
    ]
    halo_copies = [
        remote(src, dst, halo_send.at[i], halo_recv.at[i], {"freq": left})
        for i, (src, dst) in enumerate(
            [
                (nat.at[:, :, pl.ds(0, LANES)], halo),
                (gain.at[pl.ds(0, SUB)], halo_gain),
                (bins.at[pl.ds(0, SUB)], halo_bins),
            ]
        )
    ]
    for c in near_copies + halo_copies:
        c.start()

    def relay(g):
        for o in range(integ // SUB):
            slab = nat[g, o * SUB : (o + 1) * SUB, :]
            turned = jnp.transpose(
                jnp.stack([slab[:, s * width : (s + 1) * width] for s in range(SUB)]), (1, 0, 2)
            )
            for j in range(cols):
                norm[g, pl.ds(o * SUB, SUB), j] = turned[:, :, j * LANES : (j + 1) * LANES]

    relay(0)
    for c in near_copies:
        c.wait_recv()
    near_tile = tile
    for d in range(nc - 1):
        near_tile = near_tile + near[d]
    near_sum[...] = near_tile
    far_copies = [
        remote(near_sum, far.at[d], far_send.at[d], far_recv.at[d], {"freq": p})
        for d, p in enumerate(far_peers)
    ]
    for c in far_copies:
        c.start()

    for g in range(1, groups):
        relay(g)
    for c in far_copies:
        c.wait_recv()
    far_tile = near_tile
    for d in range(nz - 1):
        far_tile = far_tile + far[d]
    far_sum[...] = far_tile
    early_copies = [
        remote(far_sum, early.at[d], early_send.at[d], early_recv.at[d], {"section": p})
        for d, p in enumerate(section_peers)
    ]
    for c in early_copies:
        c.start()

    for c in halo_copies:
        c.wait_recv()
    sub = lax.broadcasted_iota(jnp.int32, (SUB, LANES), 0)
    last = sub == SUB - 1

    def past(first, row):
        return jnp.where(last, jnp.broadcast_to(row, (SUB, LANES)), pltpu.roll(first, SUB - 1, 0))

    for j in range(cols):
        ext_gain[j] = gain[pl.ds(j, SUB, stride=cols), :]
        ext_bins[j] = bins[pl.ds(j, SUB, stride=cols), :]
    ext_gain[cols] = past(ext_gain[0], halo_gain[0:1, :])
    ext_bins[cols] = past(ext_bins[0], halo_bins[0:1, :])
    for g in range(groups):
        for t in range(integ):
            norm[g, t, cols] = past(norm[g, t, 0], halo[g, t : t + 1, :])

    for c in loads[2 + groups :]:
        c.wait()
    for c in early_copies:
        c.wait_recv()
    before = jnp.zeros((SUB, LANES), F32)
    for d in range(1, ns):
        before = before + jnp.where(d <= me, early[d - 1], 0.0)
    run_low = before[0:1] + before[1:2]
    run_high = before[4:5] + before[5:6]
    wanted = jnp.logical_not(jnp.logical_and(last, here == nf - 1))
    for g in range(groups):
        run_low = run_low + far_tile[g : g + 1]
        run_high = run_high + far_tile[4 + g : 5 + g]
        order = (integ * (groups * me + g + 1)).astype(F32)
        table_low = jnp.broadcast_to(order * far_tile[2:3] / run_low, (SUB, LANES))
        table_high = jnp.broadcast_to(order * far_tile[6:7] / run_high, (SUB, LANES))
        factor = []
        for j in range(cols + 1):
            at = ext_bins[j]
            inner = jnp.bitwise_and(at, LANES - 1)
            inverse = jnp.where(
                at < LANES,
                jnp.take_along_axis(table_low, inner, axis=1),
                jnp.take_along_axis(table_high, inner, axis=1),
            )
            factor.append(ext_gain[j] * inverse)
        for t in range(integ):
            for j in range(cols):
                norm[g, t, j] = norm[g, t, j] * factor[j] - 1.0
            norm[g, t, cols] = jnp.where(wanted, norm[g, t, cols] * factor[cols] - 1.0, 0.0)

    lane = lax.broadcasted_iota(jnp.int32, (1, SUB, LANES), 2)

    def score_copy(i, dst):
        return remote(
            scores.at[i],
            out_ref.at[pl.ds(groups * me, groups)],
            score_send.at[i],
            score_recv.at[i],
            {"section": dst},
        )

    def target(i):
        m, r = i // 2, i % 2
        return (me + ns // 2 + m - r * (2 * m + 1)) % ns

    def one_stride(i, carry):
        dst = target(i)
        stride = dst + 1
        inside = [lane < LANES - n * stride for n in range(integ // 2 + 1)]

        def shifted(x, n):
            if n == 0:
                return x
            turned = pltpu.roll(x, LANES - n * stride, 2)
            kept = jnp.where(inside[n], turned[:cols], turned[1:])
            return jnp.concatenate([kept, turned[cols:]], axis=0)

        for g in range(groups):
            for q in range(integ // 4):
                x0, x1, x2, x3 = (norm[g, 4 * q + t] for t in range(4))
                u0, u1 = x0 + x1, x0 + shifted(x1, 1)
                v0, v1 = x2 + x3, x2 + shifted(x3, 1)
                quads[g, 4 * q] = u0 + v0
                quads[g, 4 * q + 1] = u0 + shifted(v0, 1)
                quads[g, 4 * q + 2] = u1 + shifted(v1, 1)
                quads[g, 4 * q + 3] = u1 + shifted(v1, 2)
            total = jnp.zeros((cols, SUB, LANES), F32)
            for h in range(integ // 2):
                a = h // 2
                first = quads[g, a] + shifted(quads[g, 4 + a], h - a)
                second = quads[g, 8 + a] + shifted(quads[g, 12 + a], h - a)
                for d in (2 * h, 2 * h + 1):
                    level = cut[g, dst, d].astype(F32) * (4.0 / 256.0)
                    drift = first[:cols] + shifted(second, d - h)[:cols]
                    total = total + jnp.maximum(drift - level, 0.0)
            weight = jnp.where(stride <= reach[groups * me + g], 0.25 / integ, 0.0)
            total = total * weight
            for j in range(cols):
                scores[i, g, pl.ds(j, SUB, stride=cols), :] = total[j]

        @pl.when(i < ns - 1)
        def _():
            score_copy(i, dst).start()

        return carry

    lax.fori_loop(0, ns, one_stride, 0)
    out_ref[pl.ds(groups * me, groups)] = scores[ns - 1]
    for i in range(ns - 1):
        score_copy(i, target(i)).wait_recv()
    for c in near_copies + halo_copies + far_copies + early_copies:
        c.wait_send()
    for i in range(ns - 1):
        score_copy(i, target(i)).wait_send()


def shards(near_count, spectra, channel_gain, bandpass_bin, drift_range, hit_cutoff):
    groups, integ, chans = spectra.shape
    ns, nf = lax.axis_size("section"), lax.axis_size("freq")
    total_bins = 2 * LANES
    nc, nz = near_count, nf // near_count
    rows, cols = chans // LANES, chans // LANES // SUB
    sizes = (ns, nf, nc, groups, integ, chans, total_bins)
    dma = pltpu.SemaphoreType.DMA
    tile = (SUB, LANES)
    out = pl.pallas_call(
        functools.partial(kernel, sizes),
        out_shape=jax.ShapeDtypeStruct((ns * groups, rows, LANES), F32),
        in_specs=[pl.BlockSpec(memory_space=pl.ANY)] * 5,
        out_specs=pl.BlockSpec(memory_space=pltpu.VMEM),
        scratch_shapes=[
            pltpu.VMEM((groups, integ, chans), F32),
            pltpu.VMEM((rows, LANES), F32),
            pltpu.VMEM((rows, LANES), jnp.int32),
            pltpu.SMEM((ns * groups,), jnp.int32),
            pltpu.SMEM((groups, *hit_cutoff.shape[1:]), jnp.int32),
            pltpu.VMEM((groups, integ, LANES), F32),
            pltpu.VMEM(tile, F32),
            pltpu.VMEM(tile, jnp.int32),
            pltpu.VMEM((cols + 1, *tile), F32),
            pltpu.VMEM((cols + 1, *tile), jnp.int32),
            pltpu.VMEM((groups, integ, cols + 1, *tile), F32),
            pltpu.VMEM((groups, integ, cols + 1, *tile), F32),
            pltpu.VMEM((ns, groups, rows, LANES), F32),
            pltpu.VMEM(tile, F32),
            pltpu.VMEM((max(nc - 1, 1), *tile), F32),
            pltpu.VMEM(tile, F32),
            pltpu.VMEM((max(nz - 1, 1), *tile), F32),
            pltpu.VMEM(tile, F32),
            pltpu.VMEM((ns - 1, *tile), F32),
            dma((4 + groups,)),
            dma((max(nc - 1, 1),)),
            dma((max(nc - 1, 1),)),
            dma((max(nz - 1, 1),)),
            dma((max(nz - 1, 1),)),
            dma((ns - 1,)),
            dma((ns - 1,)),
            dma((3,)),
            dma((3,)),
            dma((ns - 1,)),
            dma((ns - 1,)),
        ],
        compiler_params=pltpu.CompilerParams(collective_id=0, has_side_effects=True),
    )(
        spectra,
        channel_gain.reshape(rows, LANES),
        bandpass_bin.reshape(rows, LANES),
        drift_range,
        hit_cutoff,
    )
    return out.reshape(ns * groups, 1, chans)


def solution(mesh, near_count=8):
    return jax.shard_map(
        functools.partial(shards, near_count),
        mesh=mesh,
        in_specs=(P("section", None, "freq"), P("freq"), P("freq"), P(), P()),
        out_specs=P(None, "section", "freq"),
        check_vma=False,
    )
```

time: 377 us -> 47.9 us (0.13)
  the two profiles are of different devices: /device:TPU:1 before, /device:TPU:8 now
where the time goes in v1:
time: 47.9 us; the launch traced here: 47.7 us
  Pallas kernels  45.8 us (96%)
  local copies, waits for them, and re-layouts  1.89 us (4%)
    pallas_call x1, Pallas kernels, shards(): pl.pallas_call(functools.partial(kernel, sizes), out_shape=jax.ShapeDtype...  45.8 us
    unnamed x1, local copies, waits for them, and re-layouts  1.89 us

profile of v1, /device:TPU:8, one launch (start us, length us, event | category | flops | bytes accessed | tf_op | source)
XLA Modules:
  0.0 47.7 jit_solution(17452261531679361614)
XLA Ops:
  0.0 45.8 %shard_map.55 = f32[16,64,128]{2,1,0:T(8,128)} custom-call(f32[2,16,8192]{2,1,0:T(8,128)} %spec_hbm.1, f32[64,128]{1,0:T(8,128)} %bitcast.4, s32[64,128]{1,0:T(8,128)} %bitcast.5, s32[16]{0:T(128)} %reach_hbm.1, s32[16,8,16]{2,1,0:T(8,128)} %cut_hbm.1), custom_call_target="tpu_custom_call" | custom-call | tf_op jit(solution)/shard_map/pallas_call | solution.py:309
  45.9 1.9 %copy.8 = f32[16,1,8192]{2,1,0:T(1,128)} copy(f32[16,1,8192]{2,1,0:T(1,128)} %bitcast.3) | data formatting | bytes 1048576

commit v2 on v1

v2 whole, which is shorter than its diff:
```python
import functools

import jax
import jax.numpy as jnp
from jax import lax
from jax.experimental import pallas as pl
from jax.experimental.pallas import tpu as pltpu
from jax.sharding import PartitionSpec as P

F32 = jnp.float32
BF16 = jnp.bfloat16
LANES = 128
SUB = 8
MESH = pl.DeviceIdType.MESH


def remote(src, dst, send, recv, where):
    return pltpu.make_async_remote_copy(
        src_ref=src, dst_ref=dst, send_sem=send, recv_sem=recv, device_id=where, device_id_type=MESH
    )


def kernel(
    sizes,
    spec_hbm,
    gain_hbm,
    bins_hbm,
    reach_hbm,
    cut_hbm,
    out_ref,
    nat,
    gain,
    bins,
    reach,
    cut,
    halo,
    halo_gain,
    halo_bins,
    factor,
    factor_rows,
    norm,
    quads,
    total,
    scores,
    part,
    near,
    near_sum,
    far,
    far_sum,
    early,
    spec_sem,
    load_sem,
    near_send,
    near_recv,
    far_send,
    far_recv,
    early_send,
    early_recv,
    halo_send,
    halo_recv,
    score_send,
    score_recv,
):
    ns, nf, nc, groups, integ, chans, total_bins = sizes
    nz = nf // nc
    rows = chans // LANES
    wide = groups * rows
    me = lax.axis_index("section")
    here = lax.axis_index("freq")
    z, xc = here // nc, here % nc

    near_peers = [z * nc + (xc + d) % nc for d in range(1, nc)]
    far_peers = [((z + d) % nz) * nc + xc for d in range(1, nz)]
    section_peers = [(me + d) % ns for d in range(1, ns)]
    left, right = (here + nf - 1) % nf, (here + 1) % nf

    loads = [
        pltpu.make_async_copy(bins_hbm, bins, load_sem.at[0]),
        pltpu.make_async_copy(gain_hbm, gain, load_sem.at[1]),
        pltpu.make_async_copy(reach_hbm, reach, load_sem.at[2]),
        pltpu.make_async_copy(cut_hbm.at[pl.ds(groups * me, groups)], cut, load_sem.at[3]),
    ]
    spec_loads = [
        pltpu.make_async_copy(
            spec_hbm.at[g, t // SUB, :, t % SUB, :],
            nat.at[g, t, pl.ds(0, rows)],
            spec_sem.at[g * integ + t],
        )
        for g in range(groups)
        for t in range(integ)
    ]
    for c in loads[:2] + spec_loads + loads[2:]:
        c.start()

    barrier = pltpu.get_barrier_semaphore()
    for peer in near_peers + far_peers + [left, right]:
        pl.semaphore_signal(barrier, inc=1, device_id={"freq": peer}, device_id_type=MESH)
    for peer in section_peers:
        pl.semaphore_signal(barrier, inc=1, device_id={"section": peer}, device_id_type=MESH)

    bin_row = lax.broadcasted_iota(jnp.int32, (total_bins, LANES), 0)
    for c in loads[:2]:
        c.wait()
    for c in spec_loads:
        c.wait()
    acc = jnp.zeros((SUB, total_bins), F32)
    for r0 in range(0, rows, SUB):
        span = pl.ds(r0, SUB)
        high, middle, low = [], [], []
        for g in range(groups):
            value = nat[g, 0, span]
            for t in range(1, integ):
                value = value + nat[g, t, span]
            value = value * gain[span]
            high.append(value.astype(BF16).astype(F32))
            value = value - high[-1]
            middle.append(value.astype(BF16).astype(F32))
            low.append(value - middle[-1])
        ones = [jnp.ones((SUB, LANES), F32)] * 2
        turned = jnp.transpose(jnp.stack(high + middle + low + ones), (1, 0, 2))
        lhs = jnp.concatenate([turned[r] for r in range(SUB)], axis=1).astype(BF16)
        one_hot = jnp.concatenate(
            [
                (bin_row == bins[r : r + 1, :]).astype(F32).astype(BF16)
                for r in range(r0, r0 + SUB)
            ],
            axis=1,
        )
        acc = acc + lax.dot_general(
            lhs,
            one_hot,
            (((1,), (1,)), ((), ())),
            preferred_element_type=F32,
        )
    sums = acc[0:2] + acc[2:4] + acc[4:6]
    counts = acc[6:8]
    tile = jnp.concatenate(
        [sums[:, :LANES], counts[:, :LANES], sums[:, LANES:], counts[:, LANES:]], axis=0
    )
    part[...] = tile

    pl.semaphore_wait(barrier, nc + nz + ns - 1)

    near_copies = [
        remote(part, near.at[d], near_send.at[d], near_recv.at[d], {"freq": p})
        for d, p in enumerate(near_peers)
    ]
    halo_copies = [
        remote(src, dst, halo_send.at[i], halo_recv.at[i], {"freq": left})
        for i, (src, dst) in enumerate(
            [
                (nat.at[:, :, 0], halo),
                (gain.at[pl.ds(0, SUB)], halo_gain),
                (bins.at[pl.ds(0, SUB)], halo_bins),
            ]
        )
    ]
    for c in near_copies + halo_copies:
        c.start()

    def turn(t, shift):
        block = jnp.concatenate(
            [nat[g, t, pl.ds(shift, rows)] for g in range(groups)], axis=0
        )
        norm[t, pl.ds(shift * LANES, LANES)] = jnp.transpose(block)

    for t in range(integ):
        turn(t, 0)
    for c in near_copies:
        c.wait_recv()
    near_tile = tile
    for d in range(nc - 1):
        near_tile = near_tile + near[d]
    near_sum[...] = near_tile
    far_copies = [
        remote(near_sum, far.at[d], far_send.at[d], far_recv.at[d], {"freq": p})
        for d, p in enumerate(far_peers)
    ]
    for c in far_copies:
        c.start()

    for c in halo_copies:
        c.wait_recv()
    for g in range(groups):
        for t in range(integ):
            nat[g, t, pl.ds(rows, 1)] = halo[g, t : t + 1]
    for t in range(integ):
        turn(t, 1)

    for c in far_copies:
        c.wait_recv()
    far_tile = near_tile
    for d in range(nz - 1):
        far_tile = far_tile + far[d]
    far_sum[...] = far_tile
    early_copies = [
        remote(far_sum, early.at[d], early_send.at[d], early_recv.at[d], {"section": p})
        for d, p in enumerate(section_peers)
    ]
    for c in early_copies:
        c.start()

    for c in loads[2:]:
        c.wait()
    lane = lax.broadcasted_iota(jnp.int32, (SUB, wide), 1)
    ends = jnp.logical_and(lane % rows == rows - 1, here == nf - 1)
    ones_past = jnp.where(ends, 0.0, 1.0)[0:1]
    for c in early_copies:
        c.wait_recv()
    before = jnp.zeros((SUB, LANES), F32)
    for d in range(1, ns):
        before = before + jnp.where(d <= me, early[d - 1], 0.0)
    run_low = before[0:1] + before[1:2]
    run_high = before[4:5] + before[5:6]

    def looked_up(at, low, high):
        inner = jnp.bitwise_and(at, LANES - 1)
        return jnp.where(
            at < LANES,
            jnp.take_along_axis(low, inner, axis=1),
            jnp.take_along_axis(high, inner, axis=1),
        )

    for g in range(groups):
        run_low = run_low + far_tile[g : g + 1]
        run_high = run_high + far_tile[4 + g : 5 + g]
        order = (integ * (groups * me + g + 1)).astype(F32)
        low = jnp.broadcast_to(order * far_tile[2:3] / run_low, (SUB, LANES))
        high = jnp.broadcast_to(order * far_tile[6:7] / run_high, (SUB, LANES))
        for r0 in range(0, rows, SUB):
            span = pl.ds(r0, SUB)
            factor[g, span] = gain[span] * looked_up(bins[span], low, high)
        factor[g, pl.ds(rows, SUB)] = halo_gain[...] * looked_up(halo_bins[...], low, high)
    for shift in (0, 1):
        block = jnp.concatenate([factor[g, pl.ds(shift, rows)] for g in range(groups)], axis=0)
        block = jnp.transpose(block)
        if shift:
            block = block * ones_past
        factor_rows[pl.ds(shift * LANES, LANES)] = block
    reach_rows = 2 * LANES - SUB
    for t in range(integ):
        norm[t, pl.ds(0, LANES)] = norm[t, pl.ds(0, LANES)] * factor_rows[pl.ds(0, LANES)] - 1.0
        span = pl.ds(LANES, reach_rows - LANES)
        norm[t, span] = norm[t, span] * factor_rows[span] - ones_past

    def score_copy(i, dst):
        return remote(
            scores.at[i],
            out_ref.at[pl.ds(groups * me, groups)],
            score_send.at[i],
            score_recv.at[i],
            {"section": dst},
        )

    def target(i):
        m, r = i // 2, i % 2
        return (me + ns // 2 + m - r * (2 * m + 1)) % ns

    def one_stride(i, carry):
        dst = target(i)
        k = dst + 1
        first_group = lane < rows

        def by_group(values):
            return jnp.where(first_group, values[0], values[1])

        levels = [
            by_group([cut[g, dst, d].astype(F32) * (4.0 / 256.0) for g in range(groups)])
            for d in range(integ)
        ]
        weight = by_group(
            [jnp.where(k <= reach[groups * me + g], 0.25 / integ, 0.0) for g in range(groups)]
        )

        chunk = 4

        def lower(b, inner):
            for c in range(chunk):
                r = pl.multiple_of((b * chunk + c) * SUB, SUB)
                for q in range(integ // 4):

                    def x(t, n):
                        return norm[4 * q + t, pl.ds(r + n * k, SUB)]

                    x0, x10, x11 = x(0, 0), x(1, 0), x(1, 1)
                    x20, x21, x22 = x(2, 0), x(2, 1), x(2, 2)
                    x30, x31, x32, x33 = x(3, 0), x(3, 1), x(3, 2), x(3, 3)
                    u0, u1 = x0 + x10, x0 + x11
                    span = pl.ds(r, SUB)
                    quads[4 * q, span] = u0 + (x20 + x30)
                    quads[4 * q + 1, span] = u0 + (x21 + x31)
                    quads[4 * q + 2, span] = u1 + (x21 + x32)
                    quads[4 * q + 3, span] = u1 + (x22 + x33)
            return inner

        tall = chunk * SUB
        lax.fori_loop(0, (LANES + 12 * k + tall - 1) // tall, lower, 0)

        def upper(b, inner):
            for c in range(chunk):
                r = pl.multiple_of((b * chunk + c) * SUB, SUB)

                def y(row, n):
                    return quads[row, pl.ds(r + n * k, SUB)]

                sums_over = jnp.zeros((SUB, wide), F32)
                for a in range(integ // 4):
                    own = y(a, 0)
                    for h in (2 * a, 2 * a + 1):
                        e = h - a
                        first = own + y(4 + a, e)
                        for d in (2 * h, 2 * h + 1):
                            n = d - h
                            drift = first + (y(8 + a, n) + y(12 + a, n + e))
                            sums_over = sums_over + jnp.maximum(drift - levels[d], 0.0)
                total[pl.ds(r, SUB)] = sums_over * weight
            return inner

        lax.fori_loop(0, LANES // tall, upper, 0)
        turned = jnp.transpose(total[...])
        for g in range(groups):
            scores[i, g] = turned[g * rows : (g + 1) * rows]

        @pl.when(i < ns - 1)
        def _():
            score_copy(i, dst).start()

        return carry

    lax.fori_loop(0, ns, one_stride, 0)
    kept = pltpu.make_async_copy(
        scores.at[ns - 1], out_ref.at[pl.ds(groups * me, groups)], load_sem.at[0]
    )
    kept.start()
    for i in range(ns - 1):
        score_copy(i, target(i)).wait_recv()
    kept.wait()
    for c in near_copies + halo_copies + far_copies + early_copies:
        c.wait_send()
    for i in range(ns - 1):
        score_copy(i, target(i)).wait_send()


def shards(near_count, spectra, channel_gain, bandpass_bin, drift_range, hit_cutoff):
    groups, integ, chans = spectra.shape
    ns, nf = lax.axis_size("section"), lax.axis_size("freq")
    total_bins = 2 * LANES
    nc, nz = near_count, nf // near_count
    rows = chans // LANES
    wide = groups * rows
    sizes = (ns, nf, nc, groups, integ, chans, total_bins)
    dma = pltpu.SemaphoreType.DMA
    tile = (SUB, LANES)
    out = pl.pallas_call(
        functools.partial(kernel, sizes),
        out_shape=jax.ShapeDtypeStruct((ns * groups, rows, LANES), F32),
        in_specs=[pl.BlockSpec(memory_space=pltpu.HBM)] * 5,
        out_specs=pl.BlockSpec(memory_space=pl.ANY),
        scratch_shapes=[
            pltpu.VMEM((groups, integ, rows + SUB, LANES), F32),
            pltpu.VMEM((rows, LANES), F32),
            pltpu.VMEM((rows, LANES), jnp.int32),
            pltpu.SMEM((ns * groups,), jnp.int32),
            pltpu.SMEM((groups, *hit_cutoff.shape[1:]), jnp.int32),
            pltpu.VMEM((groups, integ, LANES), F32),
            pltpu.VMEM(tile, F32),
            pltpu.VMEM(tile, jnp.int32),
            pltpu.VMEM((groups, rows + SUB, LANES), F32),
            pltpu.VMEM((2 * LANES, wide), F32),
            pltpu.VMEM((integ, 2 * LANES, wide), F32),
            pltpu.VMEM((integ, 2 * LANES, wide), F32),
            pltpu.VMEM((LANES, wide), F32),
            pltpu.VMEM((ns, groups, rows, LANES), F32),
            pltpu.VMEM(tile, F32),
            pltpu.VMEM((max(nc - 1, 1), *tile), F32),
            pltpu.VMEM(tile, F32),
            pltpu.VMEM((max(nz - 1, 1), *tile), F32),
            pltpu.VMEM(tile, F32),
            pltpu.VMEM((ns - 1, *tile), F32),
            dma((groups * integ,)),
            dma((4,)),
            dma((max(nc - 1, 1),)),
            dma((max(nc - 1, 1),)),
            dma((max(nz - 1, 1),)),
            dma((max(nz - 1, 1),)),
            dma((ns - 1,)),
            dma((ns - 1,)),
            dma((3,)),
            dma((3,)),
            dma((ns - 1,)),
            dma((ns - 1,)),
        ],
        compiler_params=pltpu.CompilerParams(
            collective_id=0, has_side_effects=True, vmem_limit_bytes=16 << 20
        ),
    )(*[pltpu.with_memory_space_constraint(v, pltpu.HBM) for v in (
        spectra.reshape(groups, integ // SUB, SUB, rows, LANES).transpose(0, 1, 3, 2, 4),
        channel_gain.reshape(rows, LANES),
        bandpass_bin.reshape(rows, LANES),
        drift_range,
        hit_cutoff,
    )])
    return out.reshape(ns * groups, 1, chans)


def solution(mesh, near_count=8):
    return jax.shard_map(
        functools.partial(shards, near_count),
        mesh=mesh,
        in_specs=(P("section", None, "freq"), P("freq"), P("freq"), P(), P()),
        out_specs=P(None, "section", "freq"),
        check_vma=False,
    )
```

time: 47.9 us -> 43.3 us (0.904)
  the two profiles are of different devices: /device:TPU:8 before, /device:TPU:1 now
where the time goes in v2:
time: 43.3 us; the launch traced here: 43.1 us
  Pallas kernels  42.3 us (98%)
  local copies, waits for them, and re-layouts  0.8 us (2%)
    pallas_call x1, Pallas kernels, shards(): pl.pallas_call(functools.partial(kernel, sizes), out_shape=jax.ShapeDtype...  42.3 us

profile of v2, /device:TPU:1, one launch (start us, length us, event | category | flops | bytes accessed | tf_op | source)
XLA Modules:
  0.0 43.1 jit_solution(13251705953991163870)
XLA Ops:
  0.0 42.3 %shard_map.55 = f32[16,64,128]{2,1,0:T(8,128)S(1)} custom-call(f32[2,2,64,8,128]{4,3,2,1,0:T(8,128)} %bitcast.7, f32[64,128]{1,0:T(8,128)} %bitcast.8, s32[64,128]{1,0:T(8,128)} %bitcast.9, s32[16]{0:T(128)} %reach_hbm.1, s32[16,8,16]{2,1,0:T(8,128)} %cut_hbm.1), custom_call_target="tpu_custom_call" | custom-call | tf_op jit(solution)/shard_map/pallas_call | solution.py:354
  42.3 0.8 %copy.8 = f32[16,1,8192]{2,1,0:T(1,128)} copy(f32[16,1,8192]{2,1,0:T(1,128)S(1)} %bitcast.6) | data formatting | bytes 1048576

commit v3 on v2

--- a/solution.py
+++ b/solution.py
@@ -67,12 +67,13 @@
     wide = groups * rows
     me = lax.axis_index("section")
     here = lax.axis_index("freq")
-    z, xc = here // nc, here % nc
-
-    near_peers = [z * nc + (xc + d) % nc for d in range(1, nc)]
-    far_peers = [((z + d) % nz) * nc + xc for d in range(1, nz)]
-    section_peers = [(me + d) % ns for d in range(1, ns)]
-    left, right = (here + nf - 1) % nf, (here + 1) % nf
+    z, xc = lax.div(here, nc), lax.rem(here, nc)
+
+    at_end = here == nf - 1
+    near_peers = [z * nc + lax.rem(xc + d, nc) for d in range(1, nc)]
+    far_peers = [lax.rem(here + d * nc, nf) for d in range(1, nz)]
+    section_peers = [lax.rem(me + d, ns) for d in range(1, ns)]
+    left, right = lax.rem(here + nf - 1, nf), lax.rem(here + 1, nf)
 
     loads = [
         pltpu.make_async_copy(bins_hbm, bins, load_sem.at[0]),
@@ -89,18 +90,21 @@
         for g in range(groups)
         for t in range(integ)
     ]
-    for c in loads[:2] + spec_loads + loads[2:]:
+    for c in loads[:2] + spec_loads:
         c.start()
 
     barrier = pltpu.get_barrier_semaphore()
-    for peer in near_peers + far_peers + [left, right]:
-        pl.semaphore_signal(barrier, inc=1, device_id={"freq": peer}, device_id_type=MESH)
     for peer in section_peers:
         pl.semaphore_signal(barrier, inc=1, device_id={"section": peer}, device_id_type=MESH)
-
-    bin_row = lax.broadcasted_iota(jnp.int32, (total_bins, LANES), 0)
+    for peer in far_peers + [left, right] + near_peers:
+        pl.semaphore_signal(barrier, inc=1, device_id={"freq": peer}, device_id_type=MESH)
+
+    for c in loads[2:]:
+        c.start()
     for c in loads[:2]:
         c.wait()
+    bin_row = lax.broadcasted_iota(jnp.int32, (total_bins, LANES), 0).astype(F32).astype(BF16)
+    named = bins[...].astype(F32).astype(BF16)
     for c in spec_loads:
         c.wait()
     acc = jnp.zeros((SUB, total_bins), F32)
@@ -121,7 +125,7 @@
         lhs = jnp.concatenate([turned[r] for r in range(SUB)], axis=1).astype(BF16)
         one_hot = jnp.concatenate(
             [
-                (bin_row == bins[r : r + 1, :]).astype(F32).astype(BF16)
+                jnp.where(bin_row == named[r : r + 1], jnp.ones((), BF16), jnp.zeros((), BF16))
                 for r in range(r0, r0 + SUB)
             ],
             axis=1,
@@ -135,7 +139,7 @@
     sums = acc[0:2] + acc[2:4] + acc[4:6]
     counts = acc[6:8]
     tile = jnp.concatenate(
-        [sums[:, :LANES], counts[:, :LANES], sums[:, LANES:], counts[:, LANES:]], axis=0
+        [sums[:, :LANES], counts[:1, :LANES], sums[:, LANES:], counts[:1, LANES:]], axis=0
     )
     part[...] = tile
 
@@ -183,7 +187,7 @@
         c.wait_recv()
     for g in range(groups):
         for t in range(integ):
-            nat[g, t, pl.ds(rows, 1)] = halo[g, t : t + 1]
+            nat[g, t, pl.ds(rows, 1)] = jnp.where(at_end, 1.0, halo[g, t : t + 1])
     for t in range(integ):
         turn(t, 1)
 
@@ -192,7 +196,9 @@
     far_tile = near_tile
     for d in range(nz - 1):
         far_tile = far_tile + far[d]
-    far_sum[...] = far_tile
+    far_sum[...] = jnp.concatenate(
+        [far_tile[0:1] + far_tile[1:2], far_tile[3:4] + far_tile[4:5]], axis=0
+    )
     early_copies = [
         remote(far_sum, early.at[d], early_send.at[d], early_recv.at[d], {"section": p})
         for d, p in enumerate(section_peers)
@@ -203,15 +209,12 @@
     for c in loads[2:]:
         c.wait()
     lane = lax.broadcasted_iota(jnp.int32, (SUB, wide), 1)
-    ends = jnp.logical_and(lane % rows == rows - 1, here == nf - 1)
-    ones_past = jnp.where(ends, 0.0, 1.0)[0:1]
     for c in early_copies:
         c.wait_recv()
-    before = jnp.zeros((SUB, LANES), F32)
+    before = jnp.zeros((2, LANES), F32)
     for d in range(1, ns):
         before = before + jnp.where(d <= me, early[d - 1], 0.0)
-    run_low = before[0:1] + before[1:2]
-    run_high = before[4:5] + before[5:6]
+    run_low, run_high = before[0:1], before[1:2]
 
     def looked_up(at, low, high):
         inner = jnp.bitwise_and(at, LANES - 1)
@@ -223,25 +226,18 @@
 
     for g in range(groups):
         run_low = run_low + far_tile[g : g + 1]
-        run_high = run_high + far_tile[4 + g : 5 + g]
+        run_high = run_high + far_tile[3 + g : 4 + g]
         order = (integ * (groups * me + g + 1)).astype(F32)
         low = jnp.broadcast_to(order * far_tile[2:3] / run_low, (SUB, LANES))
-        high = jnp.broadcast_to(order * far_tile[6:7] / run_high, (SUB, LANES))
+        high = jnp.broadcast_to(order * far_tile[5:6] / run_high, (SUB, LANES))
         for r0 in range(0, rows, SUB):
             span = pl.ds(r0, SUB)
             factor[g, span] = gain[span] * looked_up(bins[span], low, high)
-        factor[g, pl.ds(rows, SUB)] = halo_gain[...] * looked_up(halo_bins[...], low, high)
+        past = halo_gain[...] * looked_up(halo_bins[...], low, high)
+        factor[g, pl.ds(rows, SUB)] = jnp.where(at_end, 1.0, past)
     for shift in (0, 1):
         block = jnp.concatenate([factor[g, pl.ds(shift, rows)] for g in range(groups)], axis=0)
-        block = jnp.transpose(block)
-        if shift:
-            block = block * ones_past
-        factor_rows[pl.ds(shift * LANES, LANES)] = block
-    reach_rows = 2 * LANES - SUB
-    for t in range(integ):
-        norm[t, pl.ds(0, LANES)] = norm[t, pl.ds(0, LANES)] * factor_rows[pl.ds(0, LANES)] - 1.0
-        span = pl.ds(LANES, reach_rows - LANES)
-        norm[t, span] = norm[t, span] * factor_rows[span] - ones_past
+        factor_rows[pl.ds(shift * LANES, LANES)] = jnp.transpose(block)
 
     def score_copy(i, dst):
         return remote(
@@ -254,7 +250,7 @@
 
     def target(i):
         m, r = i // 2, i % 2
-        return (me + ns // 2 + m - r * (2 * m + 1)) % ns
+        return lax.rem(me + ns // 2 + m - r * (2 * m + 1), ns)
 
     def one_stride(i, carry):
         dst = target(i)
@@ -265,7 +261,7 @@
             return jnp.where(first_group, values[0], values[1])
 
         levels = [
-            by_group([cut[g, dst, d].astype(F32) * (4.0 / 256.0) for g in range(groups)])
+            by_group([cut[g, dst, d].astype(F32) * (4.0 / 256.0) + integ for g in range(groups)])
             for d in range(integ)
         ]
         weight = by_group(
@@ -277,10 +273,11 @@
         def lower(b, inner):
             for c in range(chunk):
                 r = pl.multiple_of((b * chunk + c) * SUB, SUB)
+                scale = [factor_rows[pl.ds(r + n * k, SUB)] for n in range(4)]
                 for q in range(integ // 4):
 
                     def x(t, n):
-                        return norm[4 * q + t, pl.ds(r + n * k, SUB)]
+                        return norm[4 * q + t, pl.ds(r + n * k, SUB)] * scale[n]
 
                     x0, x10, x11 = x(0, 0), x(1, 0), x(1, 1)
                     x20, x21, x22 = x(2, 0), x(2, 1), x(2, 2)
@@ -332,11 +329,11 @@
         scores.at[ns - 1], out_ref.at[pl.ds(groups * me, groups)], load_sem.at[0]
     )
     kept.start()
+    for c in near_copies + halo_copies + far_copies + early_copies:
+        c.wait_send()
     for i in range(ns - 1):
         score_copy(i, target(i)).wait_recv()
     kept.wait()
-    for c in near_copies + halo_copies + far_copies + early_copies:
-        c.wait_send()
     for i in range(ns - 1):
         score_copy(i, target(i)).wait_send()
 
@@ -367,16 +364,16 @@
             pltpu.VMEM(tile, jnp.int32),
             pltpu.VMEM((groups, rows + SUB, LANES), F32),
             pltpu.VMEM((2 * LANES, wide), F32),
-            pltpu.VMEM((integ, 2 * LANES, wide), F32),
-            pltpu.VMEM((integ, 2 * LANES, wide), F32),
+            pltpu.VMEM((integ, 2 * LANES + SUB, wide), F32),
+            pltpu.VMEM((integ, 2 * LANES + SUB, wide), F32),
             pltpu.VMEM((LANES, wide), F32),
             pltpu.VMEM((ns, groups, rows, LANES), F32),
-            pltpu.VMEM(tile, F32),
-            pltpu.VMEM((max(nc - 1, 1), *tile), F32),
-            pltpu.VMEM(tile, F32),
-            pltpu.VMEM((max(nz - 1, 1), *tile), F32),
-            pltpu.VMEM(tile, F32),
-            pltpu.VMEM((ns - 1, *tile), F32),
+            pltpu.VMEM((6, LANES), F32),
+            pltpu.VMEM((max(nc - 1, 1), 6, LANES), F32),
+            pltpu.VMEM((6, LANES), F32),
+            pltpu.VMEM((max(nz - 1, 1), 6, LANES), F32),
+            pltpu.VMEM((2, LANES), F32),
+            pltpu.VMEM((ns - 1, 2, LANES), F32),
             dma((groups * integ,)),
             dma((4,)),
             dma((max(nc - 1, 1),)),

time: 43.3 us -> 42.6 us (0.984)
  Pallas kernels: 42.3 us -> 41.5 us
    pallas_call x1, Pallas kernels: 42.3 us -> 41.5 us  [shards(): pl.pallas_call(functools.partial(kernel, sizes), out_shape=jax.ShapeDtype...]
where the time goes in v3:
time: 42.6 us; the launch traced here: 42.4 us
  Pallas kernels  41.5 us (97%)
  local copies, waits for them, and re-layouts  0.8 us (2%)
    pallas_call x1, Pallas kernels, shards(): pl.pallas_call(functools.partial(kernel, sizes), out_shape=jax.ShapeDtype...  41.5 us

profile of v3, /device:TPU:1, one launch (start us, length us, event | category | flops | bytes accessed | tf_op | source)
XLA Modules:
  0.0 42.4 jit_solution(2896187893589324789)
XLA Ops:
  0.0 41.5 %shard_map.55 = f32[16,64,128]{2,1,0:T(8,128)S(1)} custom-call(f32[2,2,64,8,128]{4,3,2,1,0:T(8,128)} %bitcast.7, f32[64,128]{1,0:T(8,128)} %bitcast.8, s32[64,128]{1,0:T(8,128)} %bitcast.9, s32[16]{0:T(128)} %reach_hbm.1, s32[16,8,16]{2,1,0:T(8,128)} %cut_hbm.1), custom_call_target="tpu_custom_call" | custom-call | tf_op jit(solution)/shard_map/pallas_call | solution.py:351
  41.6 0.8 %copy.8 = f32[16,1,8192]{2,1,0:T(1,128)} copy(f32[16,1,8192]{2,1,0:T(1,128)S(1)} %bitcast.6) | data formatting | bytes 1048576

commit v4 on v3

--- a/solution.py
+++ b/solution.py
@@ -48,6 +48,9 @@
     far,
     far_sum,
     early,
+    before,
+    far_ready,
+    section_ready,
     spec_sem,
     load_sem,
     near_send,
@@ -94,9 +97,17 @@
         c.start()
 
     barrier = pltpu.get_barrier_semaphore()
-    for peer in section_peers:
-        pl.semaphore_signal(barrier, inc=1, device_id={"section": peer}, device_id_type=MESH)
-    for peer in far_peers + [left, right] + near_peers:
+    def greet(sem, cond, where):
+        @pl.when(cond)
+        def _():
+            pl.semaphore_signal(sem, inc=1, device_id=where, device_id_type=MESH)
+
+    for d, peer in enumerate(section_peers, 1):
+        greet(barrier, me + d < ns, {"section": peer})
+    for d, peer in enumerate(far_peers, 1):
+        greet(barrier, z + d < nz, {"freq": peer})
+    greet(barrier, here < nf - 1, {"freq": right})
+    for peer in near_peers:
         pl.semaphore_signal(barrier, inc=1, device_id={"freq": peer}, device_id_type=MESH)
 
     for c in loads[2:]:
@@ -143,7 +154,11 @@
     )
     part[...] = tile
 
-    pl.semaphore_wait(barrier, nc + nz + ns - 1)
+    pl.semaphore_wait(barrier, nc - 1 + z + me + jnp.where(here > 0, 1, 0))
+    for d, peer in enumerate(far_peers, 1):
+        greet(far_ready, z + d >= nz, {"freq": peer})
+    for d, peer in enumerate(section_peers, 1):
+        greet(section_ready, me + d >= ns, {"section": peer})
 
     near_copies = [
         remote(part, near.at[d], near_send.at[d], near_recv.at[d], {"freq": p})
@@ -159,8 +174,13 @@
             ]
         )
     ]
-    for c in near_copies + halo_copies:
+    for c in near_copies:
         c.start()
+
+    @pl.when(here > 0)
+    def _():
+        for c in halo_copies:
+            c.start()
 
     def turn(t, shift):
         block = jnp.concatenate(
@@ -180,17 +200,26 @@
         remote(near_sum, far.at[d], far_send.at[d], far_recv.at[d], {"freq": p})
         for d, p in enumerate(far_peers)
     ]
-    for c in far_copies:
-        c.start()
-
-    for c in halo_copies:
-        c.wait_recv()
+    for d, c in enumerate(far_copies, 1):
+        pl.when(z + d >= nz)(c.start)
+
+    @pl.when(here < nf - 1)
+    def _():
+        for c in halo_copies:
+            c.wait_recv()
+
     for g in range(groups):
         for t in range(integ):
             nat[g, t, pl.ds(rows, 1)] = jnp.where(at_end, 1.0, halo[g, t : t + 1])
     for t in range(integ):
         turn(t, 1)
 
+    @pl.when(z < nz - 1)
+    def _():
+        pl.semaphore_wait(far_ready, nz - 1 - z)
+
+    for d, c in enumerate(far_copies, 1):
+        pl.when(z + d < nz)(c.start)
     for c in far_copies:
         c.wait_recv()
     far_tile = near_tile
@@ -203,17 +232,24 @@
         remote(far_sum, early.at[d], early_send.at[d], early_recv.at[d], {"section": p})
         for d, p in enumerate(section_peers)
     ]
-    for c in early_copies:
-        c.start()
+    @pl.when(me < ns - 1)
+    def _():
+        pl.semaphore_wait(section_ready, ns - 1 - me)
+
+    for d, c in enumerate(early_copies, 1):
+        pl.when(me + d < ns)(c.start)
+    before[...] = jnp.zeros((2, LANES), F32)
 
     for c in loads[2:]:
         c.wait()
     lane = lax.broadcasted_iota(jnp.int32, (SUB, wide), 1)
-    for c in early_copies:
-        c.wait_recv()
-    before = jnp.zeros((2, LANES), F32)
-    for d in range(1, ns):
-        before = before + jnp.where(d <= me, early[d - 1], 0.0)
+    for d, c in enumerate(early_copies, 1):
+
+        @pl.when(d <= me)
+        def _():
+            c.wait_recv()
+            before[...] += early[d - 1]
+
     run_low, run_high = before[0:1], before[1:2]
 
     def looked_up(at, low, high):
@@ -239,21 +275,29 @@
         block = jnp.concatenate([factor[g, pl.ds(shift, rows)] for g in range(groups)], axis=0)
         factor_rows[pl.ds(shift * LANES, LANES)] = jnp.transpose(block)
 
-    def score_copy(i, dst):
+    def score_copy(i, off):
         return remote(
             scores.at[i],
             out_ref.at[pl.ds(groups * me, groups)],
             score_send.at[i],
-            score_recv.at[i],
-            {"section": dst},
-        )
-
-    def target(i):
-        m, r = i // 2, i % 2
-        return lax.rem(me + ns // 2 + m - r * (2 * m + 1), ns)
+            score_recv.at[off - 1],
+            {"section": lax.rem(me + off, ns)},
+        )
+
+    def plain(i):
+        m, r = lax.div(i, 2), lax.rem(i, 2)
+        return ns // 2 + m - r * (2 * m + 1)
+
+    top = lax.rem(ns - me, ns)
+    place = jnp.where(top >= ns // 2, 2 * top - ns, ns - 1 - 2 * top)
+
+    def offset(i):
+        moved = jnp.where(i == 0, top, plain(jnp.where(i <= place, i - 1, i)))
+        return jnp.where(me == 0, plain(i), moved)
 
     def one_stride(i, carry):
-        dst = target(i)
+        off = offset(i)
+        dst = lax.rem(me + off, ns)
         k = dst + 1
         first_group = lane < rows
 
@@ -320,7 +364,7 @@
 
         @pl.when(i < ns - 1)
         def _():
-            score_copy(i, dst).start()
+            score_copy(i, off).start()
 
         return carry
 
@@ -329,13 +373,21 @@
         scores.at[ns - 1], out_ref.at[pl.ds(groups * me, groups)], load_sem.at[0]
     )
     kept.start()
-    for c in near_copies + halo_copies + far_copies + early_copies:
+    for c in near_copies + far_copies:
         c.wait_send()
+
+    @pl.when(here > 0)
+    def _():
+        for c in halo_copies:
+            c.wait_send()
+
+    for d, c in enumerate(early_copies, 1):
+        pl.when(me + d < ns)(c.wait_send)
     for i in range(ns - 1):
-        score_copy(i, target(i)).wait_recv()
+        score_copy(i, i + 1).wait_recv()
     kept.wait()
     for i in range(ns - 1):
-        score_copy(i, target(i)).wait_send()
+        score_copy(i, i + 1).wait_send()
 
 
 def shards(near_count, spectra, channel_gain, bandpass_bin, drift_range, hit_cutoff):
@@ -374,6 +426,9 @@
             pltpu.VMEM((max(nz - 1, 1), 6, LANES), F32),
             pltpu.VMEM((2, LANES), F32),
             pltpu.VMEM((ns - 1, 2, LANES), F32),
+            pltpu.VMEM((2, LANES), F32),
+            pltpu.SemaphoreType.REGULAR,
+            pltpu.SemaphoreType.REGULAR,
             dma((groups * integ,)),
             dma((4,)),
             dma((max(nc - 1, 1),)),

time: 42.6 us -> 40.3 us (0.946)
  the two profiles are of different devices: /device:TPU:1 before, /device:TPU:8 now
where the time goes in v4:
time: 40.3 us; the launch traced here: 40 us
  Pallas kernels  39.2 us (97%)
  local copies, waits for them, and re-layouts  0.8 us (2%)
    pallas_call x1, Pallas kernels, shards(): pl.pallas_call(functools.partial(kernel, sizes), out_shape=jax.ShapeDtype...  39.2 us

profile of v4, /device:TPU:8, one launch (start us, length us, event | category | flops | bytes accessed | tf_op | source)
XLA Modules:
  0.0 40.0 jit_solution(12057358821174848320)
XLA Ops:
  0.0 39.2 %shard_map.55 = f32[16,64,128]{2,1,0:T(8,128)S(1)} custom-call(f32[2,2,64,8,128]{4,3,2,1,0:T(8,128)} %bitcast.7, f32[64,128]{1,0:T(8,128)} %bitcast.8, s32[64,128]{1,0:T(8,128)} %bitcast.9, s32[16]{0:T(128)} %reach_hbm.1, s32[16,8,16]{2,1,0:T(8,128)} %cut_hbm.1), custom_call_target="tpu_custom_call" | custom-call | tf_op jit(solution)/shard_map/pallas_call | solution.py:403
  39.2 0.8 %copy.8 = f32[16,1,8192]{2,1,0:T(1,128)} copy(f32[16,1,8192]{2,1,0:T(1,128)S(1)} %bitcast.6) | data formatting | bytes 1048576

commit v5 on v4

--- a/solution.py
+++ b/solution.py
@@ -284,19 +284,13 @@
             {"section": lax.rem(me + off, ns)},
         )
 
-    def plain(i):
-        m, r = lax.div(i, 2), lax.rem(i, 2)
-        return ns // 2 + m - r * (2 * m + 1)
-
-    top = lax.rem(ns - me, ns)
-    place = jnp.where(top >= ns // 2, 2 * top - ns, ns - 1 - 2 * top)
-
-    def offset(i):
-        moved = jnp.where(i == 0, top, plain(jnp.where(i <= place, i - 1, i)))
-        return jnp.where(me == 0, plain(i), moved)
-
-    def one_stride(i, carry):
-        off = offset(i)
+    orders = [2042460, 469735, 351974, 1879269, 1893724, 1893675, 1894242, 2053345]
+    order = orders[0]
+    for section in range(1, ns):
+        order = jnp.where(me == section, orders[section], order)
+
+    def one_stride(i, order):
+        off = lax.rem(order, ns)
         dst = lax.rem(me + off, ns)
         k = dst + 1
         first_group = lane < rows
@@ -366,9 +360,9 @@
         def _():
             score_copy(i, off).start()
 
-        return carry
-
-    lax.fori_loop(0, ns, one_stride, 0)
+        return lax.div(order, ns)
+
+    lax.fori_loop(0, ns, one_stride, order)
     kept = pltpu.make_async_copy(
         scores.at[ns - 1], out_ref.at[pl.ds(groups * me, groups)], load_sem.at[0]
     )

time: 40.3 us -> 40.2 us (level)
  no operation moved by 1% of the time
where the time goes in v5:
time: 40.2 us; the launch traced here: 40 us
  Pallas kernels  39.2 us (98%)
  local copies, waits for them, and re-layouts  0.8 us (2%)
    pallas_call x1, Pallas kernels, shards(): pl.pallas_call(functools.partial(kernel, sizes), out_shape=jax.ShapeDtype...  39.2 us

profile of v5, /device:TPU:8, one launch (start us, length us, event | category | flops | bytes accessed | tf_op | source)
XLA Modules:
  0.0 40.0 jit_solution(1458252003779547451)
XLA Ops:
  0.0 39.2 %shard_map.55 = f32[16,64,128]{2,1,0:T(8,128)S(1)} custom-call(f32[2,2,64,8,128]{4,3,2,1,0:T(8,128)} %bitcast.7, f32[64,128]{1,0:T(8,128)} %bitcast.8, s32[64,128]{1,0:T(8,128)} %bitcast.9, s32[16]{0:T(128)} %reach_hbm.1, s32[16,8,16]{2,1,0:T(8,128)} %cut_hbm.1), custom_call_target="tpu_custom_call" | custom-call | tf_op jit(solution)/shard_map/pallas_call | solution.py:397
  39.2 0.8 %copy.8 = f32[16,1,8192]{2,1,0:T(1,128)} copy(f32[16,1,8192]{2,1,0:T(1,128)S(1)} %bitcast.6) | data formatting | bytes 1048576

commit v6 on v5

--- a/solution.py
+++ b/solution.py
@@ -155,11 +155,6 @@
     part[...] = tile
 
     pl.semaphore_wait(barrier, nc - 1 + z + me + jnp.where(here > 0, 1, 0))
-    for d, peer in enumerate(far_peers, 1):
-        greet(far_ready, z + d >= nz, {"freq": peer})
-    for d, peer in enumerate(section_peers, 1):
-        greet(section_ready, me + d >= ns, {"section": peer})
-
     near_copies = [
         remote(part, near.at[d], near_send.at[d], near_recv.at[d], {"freq": p})
         for d, p in enumerate(near_peers)
@@ -176,6 +171,11 @@
     ]
     for c in near_copies:
         c.start()
+
+    for d, peer in enumerate(far_peers, 1):
+        greet(far_ready, z + d >= nz, {"freq": peer})
+    for d, peer in enumerate(section_peers, 1):
+        greet(section_ready, me + d >= ns, {"section": peer})
 
     @pl.when(here > 0)
     def _():

time: 40.2 us -> 40.2 us (level)
  no operation moved by 1% of the time
where the time goes in v6:
time: 40.2 us; the launch traced here: 40 us
  Pallas kernels  39.2 us (98%)
  local copies, waits for them, and re-layouts  0.8 us (2%)
    pallas_call x1, Pallas kernels, shards(): pl.pallas_call(functools.partial(kernel, sizes), out_shape=jax.ShapeDtype...  39.2 us

profile of v6, /device:TPU:8, one launch (start us, length us, event | category | flops | bytes accessed | tf_op | source)
XLA Modules:
  0.0 40.0 jit_solution(12770169384813150677)
XLA Ops:
  0.0 39.2 %shard_map.55 = f32[16,64,128]{2,1,0:T(8,128)S(1)} custom-call(f32[2,2,64,8,128]{4,3,2,1,0:T(8,128)} %bitcast.7, f32[64,128]{1,0:T(8,128)} %bitcast.8, s32[64,128]{1,0:T(8,128)} %bitcast.9, s32[16]{0:T(128)} %reach_hbm.1, s32[16,8,16]{2,1,0:T(8,128)} %cut_hbm.1), custom_call_target="tpu_custom_call" | custom-call | tf_op jit(solution)/shard_map/pallas_call | solution.py:397
  39.2 0.8 %copy.8 = f32[16,1,8192]{2,1,0:T(1,128)} copy(f32[16,1,8192]{2,1,0:T(1,128)S(1)} %bitcast.6) | data formatting | bytes 1048576
